TPU v7x, 32 devices: a whole 2x2x4 slice. The times are simulated.
32 devices in a mesh: sp: 8 (over z, y), tp: 4 (over x, core).
Axes of the slice: x: 2, y: 2, z: 4, core: 2. Of those that a mesh axis runs over, the one named last changes fastest.
Arguments:
- decay_rate: float32 [1, 4096, 4096], P(None, 'sp', 'tp'), may hold values from 0.2 to 2
- drive_in: bfloat16 [1, 4096, 4096], P(None, 'sp', 'tp'), may hold values from -6 to 6
- gate_in: bfloat16 [1, 4096, 4096], P(None, 'sp', 'tp'), may hold values from -6 to 6
- norm_gain: float32 [4096], P('tp'), may hold values from 0.25 to 1.75
Outputs:
- filtered: bfloat16 [1, 4096, 4096], P(None, 'sp', 'tp')
All inputs are finite; a program needn't handle non-finite values.
Results may differ from a plain program's by a relative error of at most 0.001.
Values sent between devices are 32-bit elements; how exact they have to be, the bound alone decides.
A program may use at most 64 MiB of HBM per device.

v0:
```python
import jax
import jax.numpy as jnp
from jax import lax
from jax.sharding import PartitionSpec as P


def prefix(value, axis, join, neutral, backward):
    count, mine = (lax.axis_size(axis), lax.axis_index(axis))
    pieces = jax.tree.map(lambda part: lax.all_gather(part, axis), value)
    if backward:
        pieces = jax.tree.map(lambda part: part[::-1], pieces)
        mine = count - 1 - mine
    total = jax.tree.map(
        lambda part, zero: jnp.full_like(part, 0) + jnp.asarray(zero, part.dtype), value, neutral
    )

    def hop(position, total):
        longer = join(total, jax.tree.map(lambda part: part[position], pieces))
        return jax.tree.map(lambda new, old: jnp.where(position < mine, new, old), longer, total)

    return lax.fori_loop(0, count - 1, hop, total)


def join_pair(earlier, later):
    return (earlier[0] * later[0], later[0] * earlier[1] + later[1])


def body(decay_rate, drive_in, gate_in, norm_gain):
    total_length = decay_rate.shape[1] * lax.axis_size("sp")
    keep = jnp.exp(-decay_rate / total_length)
    push = drive_in.astype(jnp.float32) * total_length ** (-0.5)
    product, forward = lax.associative_scan(join_pair, (keep, push), axis=1)
    entering_forward = prefix(
        (product[:, -1], forward[:, -1]),
        "sp",
        join_pair,
        (jnp.ones_like(keep[:, 0]), jnp.zeros_like(push[:, 0])),
        False,
    )
    forward = forward + product * entering_forward[1][:, None]
    product, backward = lax.associative_scan(join_pair, (keep, push), axis=1, reverse=True)
    entering_backward = prefix(
        (product[:, 0], backward[:, 0]),
        "sp",
        join_pair,
        (jnp.ones_like(keep[:, 0]), jnp.zeros_like(push[:, 0])),
        True,
    )
    backward = backward + product * entering_backward[1][:, None]
    states = forward + backward
    gated = states * jax.nn.sigmoid(gate_in.astype(jnp.float32))
    power = lax.psum(jnp.sum(gated * gated, axis=-1, keepdims=True), "tp") / (
        gated.shape[-1] * lax.axis_size("tp")
    )
    filtered = (gated * lax.rsqrt(power + 1e-06) * norm_gain).astype(jnp.bfloat16)
    return filtered


def solution(mesh):
    in_specs = (P(None, "sp", "tp"), P(None, "sp", "tp"), P(None, "sp", "tp"), P("tp"))
    out_specs = P(None, "sp", "tp")
    return jax.shard_map(body, mesh=mesh, in_specs=in_specs, out_specs=out_specs, check_vma=False)
```

profile of v0, /device:TPU:0, one launch (start us, length us, event | category | flops | bytes accessed | tf_op | source)
XLA Modules:
  0.0 348.7 jit_solution(10183357181414482121)
XLA Ops:
  5.2 8.9 %slice.633 = f32[1,256,1024]{2,1,0:T(8,128)} reverse(f32[1,256,1024]{2,1,0:T(8,128)} %slice.542), dimensions={1} | reverse | bytes 2097152 | tf_op jit(solution)/shard_map/slice | solution.py:41
  14.1 5.2 %slice.629 = f32[1,256,1024]{2,1,0:T(8,128)} reverse(f32[1,256,1024]{2,1,0:T(8,128)S(1)} %slice.546), dimensions={1} | reverse | bytes 2097152 | tf_op jit(solution)/shard_map/slice | solution.py:41
  25.0 9.1 %slice.628 = f32[1,255,1024]{2,1,0:T(8,128)} reverse(f32[1,255,1024]{2,1,0:T(8,128)} %slice.627), dimensions={1} | reverse | bytes 2088960 | tf_op jit(solution)/shard_map/slice | solution.py:41
  35.6 3.0 slice.606
  64.9 4.6 %pad.253 = f32[1,256,1024]{2,1,0:T(8,128)} pad(f32[1,128,1024]{2,1,0:T(8,128)} %add.464, f32[]{:T(128)} %constant.61.clone.1), padding=0_0_0x1_0_1x0_0_0 | pad | bytes 1572868 | tf_op jit(solution)/shard_map/pad | solution.py:32
  75.8 8.8 %pad.236 = f32[1,512,1024]{2,1,0:T(8,128)} pad(f32[1,256,1024]{2,1,0:T(8,128)} %pad_maximum_fusion, f32[]{:T(128)} %constant.61.clone.1), padding=0_0_0x0_1_1x0_0_0 | pad | bytes 3145732 | tf_op jit(solution)/shard_map/pad | solution.py:32
  84.6 4.8 %pad.237 = f32[1,512,1024]{2,1,0:T(8,128)} pad(f32[1,256,1024]{2,1,0:T(8,128)S(1)} %copy-done.6, f32[]{:T(128)} %constant.61.clone.1), padding=0_0_0x1_0_1x0_0_0 | pad | bytes 3145732 | tf_op jit(solution)/shard_map/pad | solution.py:32
  90.3 32.4 %all_gather.13 = f32[8,1,1024]{2,1,0:T(1,128)S(1)} all-gather(f32[1,1,1024]{2,1,0:T(1,128)S(1)} %slice_add_fusion.4), channel_id=1, replica_groups=mesh['sp'=8,'tp'=4] {'sp'}, dimensions={0}, use_global_device_ids=true | all-gather | bytes 36864 | tf_op jit(solution)/shard_map/all_gather | solution.py:9
  122.8 8.6 %pad.255 = f32[1,512,1024]{2,1,0:T(8,128)} pad(f32[1,256,1024]{2,1,0:T(8,128)} %add.465, f32[]{:T(128)} %constant.61.clone.1), padding=0_0_0x1_0_1x0_0_0 | pad | bytes 3145732 | tf_op jit(solution)/shard_map/pad | solution.py:32
  132.1 30.8 %all_gather.12 = f32[8,1,1024]{2,1,0:T(1,128)S(1)} all-gather(f32[1,1,1024]{2,1,0:T(1,128)S(1)} %slice_add_fusion.5), channel_id=1, replica_groups=mesh['sp'=8,'tp'=4] {'sp'}, dimensions={0}, use_global_device_ids=true | all-gather | bytes 36864 | tf_op jit(solution)/shard_map/all_gather | solution.py:9
  163.2 10.7 %reverse.9 = f32[1,512,1024]{2,1,0:T(8,128)} reverse(bf16[1,512,1024]{2,1,0:T(8,128)(2,1)S(1)} %copy-done.4), dimensions={1} | reverse | bytes 3145728 | tf_op jit(solution)/shard_map/reverse
  175.7 3.0 slice.693
  200.2 4.6 %pad.271 = f32[1,256,1024]{2,1,0:T(8,128)} pad(f32[1,128,1024]{2,1,0:T(8,128)} %add.489, f32[]{:T(128)} %constant.61.clone.1), padding=0_0_0x1_0_1x0_0_0 | pad | bytes 1572868 | tf_op jit(solution)/shard_map/pad | solution.py:41
  211.2 8.7 %pad.290 = f32[1,512,1024]{2,1,0:T(8,128)} pad(f32[1,256,1024]{2,1,0:T(8,128)} %pad_maximum_fusion.3, f32[]{:T(128)} %constant.61.clone.1), padding=0_0_0x0_1_1x0_0_0 | pad | bytes 3145732 | tf_op jit(solution)/shard_map/pad | solution.py:41
  219.9 4.8 %pad.291 = f32[1,512,1024]{2,1,0:T(8,128)} pad(f32[1,256,1024]{2,1,0:T(8,128)S(1)} %copy-done.7, f32[]{:T(128)} %constant.61.clone.1), padding=0_0_0x1_0_1x0_0_0 | pad | bytes 3145732 | tf_op jit(solution)/shard_map/pad | solution.py:41
  225.5 4.2 %add.502 = f32[1,512,1024]{2,1,0:T(8,128)} add(f32[1,512,1024]{2,1,0:T(8,128)} %pad.290, f32[1,512,1024]{2,1,0:T(8,128)} %pad.291) | non-fusion elementwise | flops 524288 | bytes 6291456 | tf_op jit(solution)/shard_map/add | solution.py:41
  229.7 16.8 %rev.18 = f32[1,512,1024]{2,1,0:T(8,128)} reverse(f32[1,512,1024]{2,1,0:T(8,128)} %add.502), dimensions={1} | reverse | bytes 4194304 | tf_op jit(solution)/shard_map/rev | solution.py:41
  246.5 30.6 %all_gather.14 = f32[8,1,1024]{2,1,0:T(1,128)S(1)} all-gather(f32[1,1,1024]{2,1,0:T(1,128)S(1)} %slice_add_fusion.1), channel_id=1, replica_groups=mesh['sp'=8,'tp'=4] {'sp'}, dimensions={0}, use_global_device_ids=true | all-gather | bytes 36864 | tf_op jit(solution)/shard_map/all_gather | solution.py:9
  277.1 4.8 %pad.273 = f32[1,512,1024]{2,1,0:T(8,128)} pad(f32[1,256,1024]{2,1,0:T(8,128)S(1)} %copy-done.5, f32[]{:T(128)} %constant.61.clone.1), padding=0_0_0x1_0_1x0_0_0 | pad | bytes 3145732 | tf_op jit(solution)/shard_map/pad | solution.py:41
  282.7 3.3 add.493
  286.0 16.8 %rev.17 = f32[1,512,1024]{2,1,0:T(8,128)} reverse(f32[1,512,1024]{2,1,0:T(8,128)} %add.493), dimensions={1} | reverse | bytes 4194304 | tf_op jit(solution)/shard_map/rev | solution.py:41
  302.8 30.6 %all_gather.15 = f32[8,1,1024]{2,1,0:T(1,128)S(1)} all-gather(f32[1,1,1024]{2,1,0:T(1,128)S(1)} %slice_add_fusion), channel_id=1, replica_groups=mesh['sp'=8,'tp'=4] {'sp'}, dimensions={0}, use_global_device_ids=true | all-gather | bytes 36864 | tf_op jit(solution)/shard_map/all_gather | solution.py:9
  333.7 6.5 %multiply_reduce_fusion = (f32[512]{0:T(512)S(1)}, f32[1,512,1024]{2,1,0:T(8,128)}) fusion(bf16[1,512,1024]{2,1,0:T(8,128)(2,1)S(1)} %copy-done.14, f32[1,512,1024]{2,1,0:T(8,128)} %rev.17, f32[1,512,1024]{2,1,0:T(8,128)} %rev.18, f32[1024]{0:T(1024)S(1)} %bitcast.28, f32[1024]{0:T(1024)S(1)} %bitcast.29, f32[1,512,1024]{2,1,0:T(8,128)S(1)} %copy-done.3, ...), kind=kLoop, calls=%fused_computation.9 | loop fusion | flops 7339520 | bytes 15738880 | tf_op jit(solution)/shard_map/reduce_sum | solution.py:52
  340.2 5.6 %psum.7 = f32[1,512,1]{1,2,0:T(1,128)S(1)} all-reduce(f32[1,512,1]{1,2,0:T(1,128)S(1)} %bitcast.31), channel_id=1, replica_groups=mesh['sp'=8,'tp'=4] {'tp'}, use_global_device_ids=true, to_apply=%region_5.6 | all-reduce | flops 512 | bytes 4096 | tf_op jit(solution)/shard_map/psum | solution.py:52
  (326 shorter events, 80.2 us)
Async XLA Ops:
  51.0 2.9 copy-start.9
  51.0 2.9 copy-start.10
  59.3 1.0 copy-start.11
  69.4 2.6 copy-start
  75.8 55.5 %copy-start.2 = (f32[1,512,1024]{2,1,0:T(8,128)}, f32[1,512,1024]{2,1,0:T(8,128)S(1)}, u32[]{:S(2)}) copy-start(f32[1,512,1024]{2,1,0:T(8,128)S(1)} %pad.254) | copy-start | bytes 6291460
  75.8 8.8 %copy-start.6 = (f32[1,256,1024]{2,1,0:T(8,128)S(1)}, f32[1,256,1024]{2,1,0:T(8,128)}, u32[]{:S(2)}) copy-start(f32[1,256,1024]{2,1,0:T(8,128)} %add.455) | copy-start | bytes 3145732
  89.5 73.7 %copy-start.4 = (bf16[1,512,1024]{2,1,0:T(8,128)(2,1)S(1)}, bf16[1,512,1024]{2,1,0:T(8,128)(2,1)}, u32[]{:S(2)}) copy-start(bf16[1,512,1024]{2,1,0:T(8,128)(2,1)} %param.9) | copy-start | bytes 3145732
  178.6 5.7 %copy-start.8 = (f32[1,256,1024]{2,1,0:T(8,128)S(1)}, f32[1,256,1024]{2,1,0:T(8,128)}, u32[]{:S(2)}) copy-start(f32[1,256,1024]{2,1,0:T(8,128)} %slice.633) | copy-start | bytes 3145732
  194.5 1.0 copy-start.12
  194.5 1.2 copy-start.13
  204.8 2.6 copy-start.1
  211.2 8.7 %copy-start.7 = (f32[1,256,1024]{2,1,0:T(8,128)S(1)}, f32[1,256,1024]{2,1,0:T(8,128)}, u32[]{:S(2)}) copy-start(f32[1,256,1024]{2,1,0:T(8,128)} %add.501) | copy-start | bytes 3145732
  229.7 47.4 %copy-start.5 = (f32[1,256,1024]{2,1,0:T(8,128)S(1)}, f32[1,256,1024]{2,1,0:T(8,128)}, u32[]{:S(2)}) copy-start(f32[1,256,1024]{2,1,0:T(8,128)} %add.491) | copy-start | bytes 3145732
  286.0 47.7 %copy-start.3 = (f32[1,512,1024]{2,1,0:T(8,128)S(1)}, f32[1,512,1024]{2,1,0:T(8,128)}, u32[]{:S(2)}) copy-start(f32[1,512,1024]{2,1,0:T(8,128)} %copy-done.2) | copy-start | bytes 6291460
  286.0 47.7 %copy-start.14 = (bf16[1,512,1024]{2,1,0:T(8,128)(2,1)S(1)}, bf16[1,512,1024]{2,1,0:T(8,128)(2,1)}, u32[]{:S(2)}) copy-start(bf16[1,512,1024]{2,1,0:T(8,128)(2,1)} %param.10) | copy-start | bytes 3145732
  333.7 12.2 %copy-start.15 = (f32[1024]{0:T(1024)S(1)}, f32[1024]{0:T(1024)}, u32[]{:S(2)}) copy-start(f32[1024]{0:T(1024)} %param.11) | copy-start | bytes 12292
where the time goes:
time: 353 us; the launch traced here: 349 us
  local copies, waits for them, and re-layouts  167 us (47%)
  blocking collectives  130 us (37%)
  other arithmetic  49.3 us (14%)
    all_gather x4, blocking collectives, prefix(): pieces = jax.tree.map(lambda part: lax.all_gather(part, axis), value)  124 us
    slice x60, local copies, waits for them, and re-layouts, body(): lax.associative_scan(join_pair, (keep, push), axis=1, reverse=True)  40.6 us
    rev x2, local copies, waits for them, and re-layouts, body(): lax.associative_scan(join_pair, (keep, push), axis=1, reverse=True)  33.6 us
    pad x32, local copies, waits for them, and re-layouts, body(): product, forward = lax.associative_scan(join_pair, (keep, push), axis=1)  30.2 us
    pad x32, local copies, waits for them, and re-layouts, body(): lax.associative_scan(join_pair, (keep, push), axis=1, reverse=True)  26.3 us
    slice x60, local copies, waits for them, and re-layouts, body(): product, forward = lax.associative_scan(join_pair, (keep, push), axis=1)  24.5 us
    add x19, other arithmetic, body(): lax.associative_scan(join_pair, (keep, push), axis=1, reverse=True)  13.1 us
    another operation x1, local copies, waits for them, and re-layouts  10.7 us

commit v1 on v0

v1 whole, which is shorter than its diff:
```python
import functools

import jax
import jax.numpy as jnp
from jax import lax
from jax.experimental import pallas as pl
from jax.experimental.pallas import tpu as pltpu
from jax.sharding import PartitionSpec as P

LANES = 128
SUB = 8
LOG2E = 1.4426950408889634
MESH = pl.DeviceIdType.MESH


def unrolled(count, by, step, carry):
    by = next(size for size in range(min(by, count), 0, -1) if count % size == 0)

    def block(outer, carry):
        for inner in range(by):
            carry = step(outer * by + inner, carry)
        return carry

    return lax.fori_loop(0, count // by, block, carry)


def kernel(
    nsp, ntp, decay, drive, gate, gain, out,
    decay_v, drive_v, gate_v, keep_s, push_s, sig_s, fwd_s, pre_s, suf_s, gated_s,
    inv_s, edge_s, totals, powers, in_sem, tsend, trecv, psend, precv,
):
    rows, channels = decay.shape
    tiles = channels // LANES
    steps = rows // SUB
    length = rows * nsp
    me, mine = lax.axis_index("sp"), lax.axis_index("tp")

    copies = []
    for kind, (source, held) in enumerate(((decay, decay_v), (drive, drive_v), (gate, gate_v))):
        copies.append([
            pltpu.make_async_copy(
                source.at[:, pl.ds(j * LANES, LANES)], held.at[j], in_sem.at[kind, j]
            )
            for j in range(tiles)
        ])
    for j in range(tiles):
        copies[0][j].start()
        copies[1][j].start()
    for j in range(tiles):
        copies[2][j].start()

    barrier = pltpu.get_barrier_semaphore()
    for d in range(1, nsp):
        pl.semaphore_signal(barrier, inc=1, device_id={"sp": lax.rem(me + d, nsp)}, device_id_type=MESH)
    for d in range(1, ntp):
        pl.semaphore_signal(barrier, inc=1, device_id={"tp": lax.rem(mine + d, ntp)}, device_id_type=MESH)

    row = lax.broadcasted_iota(jnp.int32, (SUB, LANES), 0)
    zero = jnp.zeros((SUB, LANES), jnp.float32)
    one = jnp.ones((SUB, LANES), jnp.float32)

    def at(k):
        return pl.ds(k, SUB, stride=steps)

    def packed(k):
        return pl.ds(pl.multiple_of(k * SUB, SUB), SUB)

    group = min(4, tiles)
    for first in range(0, tiles, group):
        members = range(first, min(first + group, tiles))
        for j in members:
            copies[0][j].wait()
            copies[1][j].wait()
            push_s[j] = drive_v[j].astype(jnp.float32)

        def ahead(k, carry):
            after = []
            for j, (prod, fwd, bwd) in zip(members, carry):
                keep = jnp.exp2(decay_v[j, at(k), :] * (-LOG2E / length))
                push = push_s[j, at(k), :]
                bwd = bwd + prod * push
                prod = prod * keep
                fwd = keep * fwd + push
                keep_s[j, packed(k), :] = keep
                fwd_s[j, packed(k), :] = fwd
                pre_s[j, packed(k), :] = prod
                after.append((prod, fwd, bwd))
            return tuple(after)

        ends = unrolled(steps, 8, ahead, tuple((one, zero, zero) for _ in members))
        for j, (prod, fwd, bwd) in zip(members, ends):
            whole, span = prod, prod
            for s in (1, 2, 4):
                keeps = row >= s
                fwd = fwd + whole * jnp.where(keeps, pltpu.roll(fwd, s, 0), 0.0)
                whole = whole * jnp.where(keeps, pltpu.roll(whole, s, 0), 1.0)
                keeps = row < SUB - s
                bwd = bwd + span * jnp.where(keeps, pltpu.roll(bwd, SUB - s, 0), 0.0)
                span = span * jnp.where(keeps, pltpu.roll(span, SUB - s, 0), 1.0)
            totals[me, 0, pl.ds(j, 1), :] = bwd[:1]
            totals[me, 1, pl.ds(j, 1), :] = whole[SUB - 1 :]
            totals[me, 2, pl.ds(j, 1), :] = fwd[SUB - 1 :]
            edge_s[0, j] = jnp.where(row >= 1, pltpu.roll(whole, 1, 0), 1.0)
            edge_s[1, j] = jnp.where(row >= 1, pltpu.roll(fwd, 1, 0), 0.0)
            edge_s[2, j] = jnp.where(row < SUB - 1, pltpu.roll(span, SUB - 1, 0), 1.0)
            edge_s[3, j] = jnp.where(row < SUB - 1, pltpu.roll(bwd, SUB - 1, 0), 0.0)

    pl.semaphore_wait(barrier, nsp + ntp - 2)

    sends = []
    for d in range(1, nsp):
        part = pl.ds(1 - (me + d) // nsp, 2)
        sends.append(pltpu.make_async_remote_copy(
            src_ref=totals.at[me, part],
            dst_ref=totals.at[me, part],
            send_sem=tsend.at[d],
            recv_sem=trecv.at[d],
            device_id={"sp": lax.rem(me + d, nsp)},
            device_id_type=MESH,
        ))
    for copy in sends:
        copy.start()

    for j in range(tiles):
        copies[2][j].wait()

        def squash(k, carry):
            here = pl.ds(pl.multiple_of(k * 2 * SUB, 2 * SUB), 2 * SUB)
            value = gate_v[j, here, :].astype(jnp.float32)
            sig_s[j, here, :] = 1.0 / (1.0 + jnp.exp2(value * -LOG2E))
            return carry

        unrolled(rows // (2 * SUB), 8, squash, 0)

    for first in range(0, tiles, group):
        members = range(first, min(first + group, tiles))

        def astern(i, carry):
            k = steps - 1 - i
            after = []
            for j, (prod, bwd) in zip(members, carry):
                keep = keep_s[j, packed(k), :]
                bwd = keep * bwd + push_s[j, at(k), :]
                prod = keep * prod
                sig = sig_s[j, at(k), :]
                fwd_s[j, packed(k), :] = (fwd_s[j, packed(k), :] + bwd) * sig
                pre_s[j, packed(k), :] = pre_s[j, packed(k), :] * sig
                suf_s[j, packed(k), :] = prod * sig
                after.append((prod, bwd))
            return tuple(after)

        unrolled(steps, 8, astern, tuple((one, zero) for _ in members))

    for copy in sends:
        copy.wait()

    enter_f = jnp.zeros((tiles, LANES), jnp.float32)
    enter_b = jnp.zeros((tiles, LANES), jnp.float32)
    for s in range(nsp - 1):
        enter_f = jnp.where(s < me, totals[s, 1] * enter_f + totals[s, 2], enter_f)
        e = nsp - 1 - s
        enter_b = jnp.where(e > me, totals[e, 1] * enter_b + totals[e, 0], enter_b)
    start_f = [edge_s[0, j] * enter_f[j : j + 1] + edge_s[1, j] for j in range(tiles)]
    start_b = [edge_s[2, j] * enter_b[j : j + 1] + edge_s[3, j] for j in range(tiles)]

    width = powers.shape[-1]
    lane = lax.broadcasted_iota(jnp.int32, (SUB, width), 1)

    def finish(k, sums):
        squares = zero
        for j in range(tiles):
            gated = (
                fwd_s[j, packed(k), :]
                + pre_s[j, packed(k), :] * start_f[j]
                + suf_s[j, packed(k), :] * start_b[j]
            )
            gated_s[j, at(k), :] = gated
            squares = squares + gated * gated
        return jnp.where(lane == k, jnp.sum(squares, axis=1, keepdims=True), sums)

    powers[mine] = unrolled(steps, 8, finish, jnp.zeros((SUB, width), jnp.float32))

    sends = []
    for d in range(1, ntp):
        sends.append(pltpu.make_async_remote_copy(
            src_ref=powers.at[mine],
            dst_ref=powers.at[mine],
            send_sem=psend.at[d],
            recv_sem=precv.at[d],
            device_id={"tp": lax.rem(mine + d, ntp)},
            device_id_type=MESH,
        ))
    for copy in sends:
        copy.start()
    for copy in sends:
        copy.wait()

    power = powers[0]
    for s in range(1, ntp):
        power = power + powers[s]
    power = power * (1.0 / (length * channels * ntp))
    inverse = lax.rsqrt(power + 1e-06) * length ** (-0.5)
    for k in range(steps):
        inv_s[at(k), :] = jnp.broadcast_to(inverse[:, k : k + 1], (SUB, LANES))

    gains = [gain[j : j + 1, :] for j in range(tiles)]

    def emit(k, carry):
        here = pl.ds(pl.multiple_of(k * 2 * SUB, 2 * SUB), 2 * SUB)
        scale = inv_s[here, :]
        for j in range(tiles):
            out[here, pl.ds(j * LANES, LANES)] = (
                gated_s[j, here, :] * scale * gains[j]
            ).astype(jnp.bfloat16)
        return carry

    unrolled(rows // (2 * SUB), 4, emit, 0)


def body(nsp, ntp, decay_rate, drive_in, gate_in, norm_gain):
    batch, rows, channels = decay_rate.shape
    tiles = channels // LANES
    steps = rows // SUB
    width = -(-steps // LANES) * LANES
    plane = pltpu.VMEM((tiles, rows, LANES), jnp.float32)
    half = pltpu.VMEM((tiles, rows, LANES), jnp.bfloat16)
    anywhere = pl.BlockSpec(memory_space=pl.ANY)
    vmem = pl.BlockSpec(memory_space=pltpu.VMEM)
    result = pl.pallas_call(
        functools.partial(kernel, nsp, ntp),
        out_shape=jax.ShapeDtypeStruct((rows, channels), jnp.bfloat16),
        in_specs=[anywhere, anywhere, anywhere, vmem],
        out_specs=vmem,
        scratch_shapes=[
            plane, half, half, plane, plane, plane, plane, plane, plane, plane,
            pltpu.VMEM((rows, LANES), jnp.float32),
            pltpu.VMEM((4, tiles, SUB, LANES), jnp.float32),
            pltpu.VMEM((nsp, 3, tiles, LANES), jnp.float32),
            pltpu.VMEM((ntp, SUB, width), jnp.float32),
            pltpu.SemaphoreType.DMA((3, tiles)),
            pltpu.SemaphoreType.DMA((nsp,)),
            pltpu.SemaphoreType.DMA((nsp,)),
            pltpu.SemaphoreType.DMA((ntp,)),
            pltpu.SemaphoreType.DMA((ntp,)),
        ],
        compiler_params=pltpu.CompilerParams(collective_id=0, has_side_effects=True),
    )(
        decay_rate.reshape(rows, channels),
        drive_in.reshape(rows, channels),
        gate_in.reshape(rows, channels),
        norm_gain.reshape(tiles, LANES),
    )
    return result.reshape(batch, rows, channels)


def solution(mesh):
    in_specs = (P(None, "sp", "tp"), P(None, "sp", "tp"), P(None, "sp", "tp"), P("tp"))
    out_specs = P(None, "sp", "tp")
    local = functools.partial(body, mesh.shape["sp"], mesh.shape["tp"])
    return jax.shard_map(local, mesh=mesh, in_specs=in_specs, out_specs=out_specs, check_vma=False)
```

time: 353 us -> 23.1 us (0.07); the launches traced: 349 us -> 22.9 us
  local copies, waits for them, and re-layouts: 167 us -> 2.26 us
  blocking collectives: 130 us -> 0 us
  other arithmetic: 49.3 us -> 0 us
  Pallas kernels: 0 us -> 20.6 us
    all_gather x4 -> x0, blocking collectives: 124 us -> none  [prefix(): pieces = jax.tree.map(lambda part: lax.all_gather(part, axis), value)]
    slice x120 -> x0, local copies, waits for them, and re-layouts: 65.1 us -> none  [the longest x60 40.6 us: body(): lax.associative_scan(join_pair, (keep, push), axis=1, reverse=True)]
    pad x64 -> x0, local copies, waits for them, and re-layouts: 56.5 us -> none  [the longest x32 30.2 us: body(): product, forward = lax.associative_scan(join_pair, (keep, push), axis=1)]
    rev x4 -> x0, local copies, waits for them, and re-layouts: 33.6 us -> none  [the longest x2 33.6 us: body(): lax.associative_scan(join_pair, (keep, push), axis=1, reverse=True)]
    add x51 -> x0, other arithmetic: 25.7 us -> none  [the longest x19 13.1 us: body(): lax.associative_scan(join_pair, (keep, push), axis=1, reverse=True)]
    pallas_call x0 -> x1, Pallas kernels: none -> 20.6 us  [body(): pl.pallas_call(functools.partial(kernel, nsp, ntp), out_shape=jax.ShapeDt...]
    another operation x1 -> x0, local copies, waits for them, and re-layouts: 10.7 us -> none
    mul x17 -> x0, other arithmetic: 7.24 us -> none  [the longest x16 5.76 us: join_pair(): return (earlier[0] * later[0], later[0] * earlier[1] + later[1])]
where the time goes in v1:
time: 23.1 us; the launch traced here: 22.9 us
  Pallas kernels  20.6 us (89%)
  local copies, waits for them, and re-layouts  2.26 us (10%)
    pallas_call x1, Pallas kernels, body(): pl.pallas_call(functools.partial(kernel, nsp, ntp), out_shape=jax.ShapeDt...  20.6 us
    unnamed x1, local copies, waits for them, and re-layouts  2.26 us

profile of v1, /device:TPU:0, one launch (start us, length us, event | category | flops | bytes accessed | tf_op | source)
XLA Modules:
  0.0 22.9 jit_solution(1440632208238067933)
XLA Ops:
  0.0 20.6 %shard_map.46 = bf16[512,1024]{1,0:T(8,128)(2,1)} custom-call(f32[512,1024]{1,0:T(8,128)} %bitcast.6, bf16[512,1024]{1,0:T(8,128)(2,1)} %bitcast.7, bf16[512,1024]{1,0:T(8,128)(2,1)} %bitcast.8, f32[8,128]{1,0:T(8,128)} %bitcast.9), custom_call_target="tpu_custom_call" | custom-call | tf_op jit(solution)/shard_map/pallas_call | solution.py:229
  20.6 2.3 %copy.6 = bf16[1,512,1024]{2,1,0:T(8,128)(2,1)} copy(bf16[1,512,1024]{2,1,0:T(8,128)(2,1)} %bitcast.5) | data formatting | bytes 2097152

commit v2 on v1

--- a/solution.py
+++ b/solution.py
@@ -24,15 +24,20 @@
     return lax.fori_loop(0, count // by, block, carry)
 
 
+def spaced(steps):
+    return steps + next(more for more in range(4, 40, 4) if (steps + more) % 8 == 4)
+
+
 def kernel(
     nsp, ntp, decay, drive, gate, gain, out,
-    decay_v, drive_v, gate_v, keep_s, push_s, sig_s, fwd_s, pre_s, suf_s, gated_s,
-    inv_s, edge_s, totals, powers, in_sem, tsend, trecv, psend, precv,
+    decay_v, drive_v, gate_v, decay_s, push_s, sig_s, fwd_s, pre_s, suf_s, gated_s,
+    inv_s, edge_s, totals, powers, gain_v, gain_sem, in_sem, tsend, trecv, psend, precv,
 ):
     rows, channels = decay.shape
     tiles = channels // LANES
     steps = rows // SUB
     length = rows * nsp
+    pitch = spaced(steps)
     me, mine = lax.axis_index("sp"), lax.axis_index("tp")
 
     copies = []
@@ -48,6 +53,8 @@
         copies[1][j].start()
     for j in range(tiles):
         copies[2][j].start()
+    gain_copy = pltpu.make_async_copy(gain, gain_v, gain_sem)
+    gain_copy.start()
 
     barrier = pltpu.get_barrier_semaphore()
     for d in range(1, nsp):
@@ -60,7 +67,11 @@
     one = jnp.ones((SUB, LANES), jnp.float32)
 
     def at(k):
-        return pl.ds(k, SUB, stride=steps)
+        return pl.ds(k, SUB, stride=pitch)
+
+    chunks = [
+        (pl.ds(i * steps, steps), pl.ds(i * pitch, steps)) for i in range(SUB)
+    ]
 
     def packed(k):
         return pl.ds(pl.multiple_of(k * SUB, SUB), SUB)
@@ -71,17 +82,18 @@
         for j in members:
             copies[0][j].wait()
             copies[1][j].wait()
-            push_s[j] = drive_v[j].astype(jnp.float32)
+            for dense, apart in chunks:
+                decay_s[j, apart, :] = jnp.exp2(decay_v[j, dense, :] * (-LOG2E / length))
+                push_s[j, apart, :] = drive_v[j, dense, :].astype(jnp.float32)
 
         def ahead(k, carry):
             after = []
             for j, (prod, fwd, bwd) in zip(members, carry):
-                keep = jnp.exp2(decay_v[j, at(k), :] * (-LOG2E / length))
+                keep = decay_s[j, at(k), :]
                 push = push_s[j, at(k), :]
                 bwd = bwd + prod * push
                 prod = prod * keep
                 fwd = keep * fwd + push
-                keep_s[j, packed(k), :] = keep
                 fwd_s[j, packed(k), :] = fwd
                 pre_s[j, packed(k), :] = prod
                 after.append((prod, fwd, bwd))
@@ -124,13 +136,9 @@
     for j in range(tiles):
         copies[2][j].wait()
 
-        def squash(k, carry):
-            here = pl.ds(pl.multiple_of(k * 2 * SUB, 2 * SUB), 2 * SUB)
-            value = gate_v[j, here, :].astype(jnp.float32)
-            sig_s[j, here, :] = 1.0 / (1.0 + jnp.exp2(value * -LOG2E))
-            return carry
-
-        unrolled(rows // (2 * SUB), 8, squash, 0)
+        for dense, apart in chunks:
+            value = gate_v[j, dense, :].astype(jnp.float32)
+            sig_s[j, apart, :] = 1.0 / (1.0 + jnp.exp2(value * -LOG2E))
 
     for first in range(0, tiles, group):
         members = range(first, min(first + group, tiles))
@@ -139,7 +147,7 @@
             k = steps - 1 - i
             after = []
             for j, (prod, bwd) in zip(members, carry):
-                keep = keep_s[j, packed(k), :]
+                keep = decay_s[j, at(k), :]
                 bwd = keep * bwd + push_s[j, at(k), :]
                 prod = keep * prod
                 sig = sig_s[j, at(k), :]
@@ -203,18 +211,16 @@
     for k in range(steps):
         inv_s[at(k), :] = jnp.broadcast_to(inverse[:, k : k + 1], (SUB, LANES))
 
-    gains = [gain[j : j + 1, :] for j in range(tiles)]
-
-    def emit(k, carry):
-        here = pl.ds(pl.multiple_of(k * 2 * SUB, 2 * SUB), 2 * SUB)
-        scale = inv_s[here, :]
-        for j in range(tiles):
-            out[here, pl.ds(j * LANES, LANES)] = (
-                gated_s[j, here, :] * scale * gains[j]
-            ).astype(jnp.bfloat16)
+    gain_copy.wait()
+
+    def emit(j, carry):
+        columns = pl.ds(pl.multiple_of(j * LANES, LANES), LANES)
+        own = gain_v[pl.ds(j, 1), :]
+        for dense, apart in chunks:
+            out[dense, columns] = (gated_s[j, apart, :] * inv_s[apart, :] * own).astype(jnp.bfloat16)
         return carry
 
-    unrolled(rows // (2 * SUB), 4, emit, 0)
+    lax.fori_loop(0, tiles, emit, 0)
 
 
 def body(nsp, ntp, decay_rate, drive_in, gate_in, norm_gain):
@@ -223,27 +229,32 @@
     steps = rows // SUB
     width = -(-steps // LANES) * LANES
     plane = pltpu.VMEM((tiles, rows, LANES), jnp.float32)
+    wide = pltpu.VMEM((tiles, SUB * spaced(steps), LANES), jnp.float32)
     half = pltpu.VMEM((tiles, rows, LANES), jnp.bfloat16)
-    anywhere = pl.BlockSpec(memory_space=pl.ANY)
+    outside = pl.BlockSpec(memory_space=pltpu.HBM)
     vmem = pl.BlockSpec(memory_space=pltpu.VMEM)
     result = pl.pallas_call(
         functools.partial(kernel, nsp, ntp),
         out_shape=jax.ShapeDtypeStruct((rows, channels), jnp.bfloat16),
-        in_specs=[anywhere, anywhere, anywhere, vmem],
+        in_specs=[outside] * 4,
         out_specs=vmem,
         scratch_shapes=[
-            plane, half, half, plane, plane, plane, plane, plane, plane, plane,
-            pltpu.VMEM((rows, LANES), jnp.float32),
+            plane, half, half, wide, wide, wide, plane, plane, plane, wide,
+            pltpu.VMEM((SUB * spaced(steps), LANES), jnp.float32),
             pltpu.VMEM((4, tiles, SUB, LANES), jnp.float32),
             pltpu.VMEM((nsp, 3, tiles, LANES), jnp.float32),
             pltpu.VMEM((ntp, SUB, width), jnp.float32),
+            pltpu.VMEM((tiles, LANES), jnp.float32),
+            pltpu.SemaphoreType.DMA,
             pltpu.SemaphoreType.DMA((3, tiles)),
             pltpu.SemaphoreType.DMA((nsp,)),
             pltpu.SemaphoreType.DMA((nsp,)),
             pltpu.SemaphoreType.DMA((ntp,)),
             pltpu.SemaphoreType.DMA((ntp,)),
         ],
-        compiler_params=pltpu.CompilerParams(collective_id=0, has_side_effects=True),
+        compiler_params=pltpu.CompilerParams(
+            collective_id=0, has_side_effects=True, vmem_limit_bytes=52 * 1024 * 1024
+        ),
     )(
         decay_rate.reshape(rows, channels),
         drive_in.reshape(rows, channels),

time: 23.1 us -> 16.9 us (0.73)
  Pallas kernels: 20.6 us -> 15.1 us
  local copies, waits for them, and re-layouts: 2.26 us -> 1.66 us
    pallas_call x1, Pallas kernels: 20.6 us -> 15.1 us  [body(): pl.pallas_call(functools.partial(kernel, nsp, ntp), out_shape=jax.ShapeDt...]
    unnamed x1 -> x3, local copies, waits for them, and re-layouts: 2.26 us -> 1.66 us
where the time goes in v2:
time: 16.9 us; the launch traced here: 16.7 us
  Pallas kernels  15.1 us (89%)
  local copies, waits for them, and re-layouts  1.66 us (10%)
    pallas_call x1, Pallas kernels, body(): pl.pallas_call(functools.partial(kernel, nsp, ntp), out_shape=jax.ShapeDt...  15.1 us
    unnamed x3, local copies, waits for them, and re-layouts  1.66 us

profile of v2, /device:TPU:0, one launch (start us, length us, event | category | flops | bytes accessed | tf_op | source)
XLA Modules:
  0.0 16.7 jit_solution(7993530523791191074)
XLA Ops:
  0.0 0.0 copy-start
  0.0 0.7 %copy-done = f32[1024]{0:T(1024)S(1)} copy-done((f32[1024]{0:T(1024)S(1)}, f32[1024]{0:T(1024)}, u32[]{:S(2)}) %copy-start) | copy-done | bytes 4120
  0.7 15.1 %shard_map.46 = bf16[512,1024]{1,0:T(8,128)(2,1)S(1)} custom-call(f32[512,1024]{1,0:T(8,128)} %bitcast.7, bf16[512,1024]{1,0:T(8,128)(2,1)} %bitcast.8, bf16[512,1024]{1,0:T(8,128)(2,1)} %bitcast.9, f32[8,128]{1,0:T(8,128)S(1)} %bitcast.6), custom_call_target="tpu_custom_call" | custom-call | tf_op jit(solution)/shard_map/pallas_call | solution.py:236
  15.8 1.0 %copy.6 = bf16[1,512,1024]{2,1,0:T(8,128)(2,1)} copy(bf16[1,512,1024]{2,1,0:T(8,128)(2,1)S(1)} %bitcast.5) | data formatting | bytes 2097152
Async XLA Ops:
  0.0 0.7 %copy-start = (f32[1024]{0:T(1024)S(1)}, f32[1024]{0:T(1024)}, u32[]{:S(2)}) copy-start(f32[1024]{0:T(1024)} %param.7) | copy-start | bytes 12292

commit v3 on v2

--- a/solution.py
+++ b/solution.py
@@ -120,14 +120,19 @@
     pl.semaphore_wait(barrier, nsp + ntp - 2)
 
     sends = []
-    for d in range(1, nsp):
+    ahead_first = (2 * me + 1) // nsp
+    for i in range(nsp - 1):
+        high = nsp - 1 - i - (i + me + 1) // nsp
+        low = i + (nsp - 1 - me + i + 1) // nsp
+        peer = high * (1 - ahead_first) + low * ahead_first
+        d = lax.rem(peer - me + nsp, nsp)
         part = pl.ds(1 - (me + d) // nsp, 2)
         sends.append(pltpu.make_async_remote_copy(
             src_ref=totals.at[me, part],
             dst_ref=totals.at[me, part],
             send_sem=tsend.at[d],
             recv_sem=trecv.at[d],
-            device_id={"sp": lax.rem(me + d, nsp)},
+            device_id={"sp": peer},
             device_id_type=MESH,
         ))
     for copy in sends:
@@ -255,12 +260,15 @@
         compiler_params=pltpu.CompilerParams(
             collective_id=0, has_side_effects=True, vmem_limit_bytes=52 * 1024 * 1024
         ),
-    )(
-        decay_rate.reshape(rows, channels),
-        drive_in.reshape(rows, channels),
-        gate_in.reshape(rows, channels),
-        norm_gain.reshape(tiles, LANES),
-    )
+    )(*(
+        pltpu.with_memory_space_constraint(value, pltpu.HBM)
+        for value in (
+            decay_rate.reshape(rows, channels),
+            drive_in.reshape(rows, channels),
+            gate_in.reshape(rows, channels),
+            norm_gain.reshape(tiles, LANES),
+        )
+    ))
     return result.reshape(batch, rows, channels)
 
 

time: 16.9 us -> 16.2 us (0.959)
  local copies, waits for them, and re-layouts: 1.66 us -> 0.97 us
    unnamed x3 -> x1, local copies, waits for them, and re-layouts: 1.66 us -> 0.97 us
where the time goes in v3:
time: 16.2 us; the launch traced here: 16.1 us
  Pallas kernels  15.1 us (93%)
  local copies, waits for them, and re-layouts  0.97 us (6%)
    pallas_call x1, Pallas kernels, body(): pl.pallas_call(functools.partial(kernel, nsp, ntp), out_shape=jax.ShapeDt...  15.1 us
    unnamed x1, local copies, waits for them, and re-layouts  0.97 us

profile of v3, /device:TPU:0, one launch (start us, length us, event | category | flops | bytes accessed | tf_op | source)
XLA Modules:
  0.0 16.1 jit_solution(6848451446046982897)
XLA Ops:
  0.0 15.1 %shard_map.46 = bf16[512,1024]{1,0:T(8,128)(2,1)S(1)} custom-call(f32[512,1024]{1,0:T(8,128)} %bitcast.6, bf16[512,1024]{1,0:T(8,128)(2,1)} %bitcast.7, bf16[512,1024]{1,0:T(8,128)(2,1)} %bitcast.8, f32[8,128]{1,0:T(8,128)} %bitcast.9), custom_call_target="tpu_custom_call" | custom-call | tf_op jit(solution)/shard_map/pallas_call | solution.py:241
  15.1 1.0 %copy.6 = bf16[1,512,1024]{2,1,0:T(8,128)(2,1)} copy(bf16[1,512,1024]{2,1,0:T(8,128)(2,1)S(1)} %bitcast.5) | data formatting | bytes 2097152

commit v4 on v3

--- a/solution.py
+++ b/solution.py
@@ -29,9 +29,9 @@
 
 
 def kernel(
-    nsp, ntp, decay, drive, gate, gain, out,
-    decay_v, drive_v, gate_v, decay_s, push_s, sig_s, fwd_s, pre_s, suf_s, gated_s,
-    inv_s, edge_s, totals, powers, gain_v, gain_sem, in_sem, tsend, trecv, psend, precv,
+    nsp, ntp, decay, drive, gate, gain, gated_s, inverse,
+    decay_v, drive_v, gate_v, decay_s, push_s, sig_s, fwd_s, pre_s, suf_s,
+    edge_s, totals, powers, gain_v, gain_sem, in_sem, tsend, trecv, psend, precv,
 ):
     rows, channels = decay.shape
     tiles = channels // LANES
@@ -39,6 +39,12 @@
     length = rows * nsp
     pitch = spaced(steps)
     me, mine = lax.axis_index("sp"), lax.axis_index("tp")
+
+    barrier = pltpu.get_barrier_semaphore()
+    for d in range(1, nsp):
+        pl.semaphore_signal(barrier, inc=1, device_id={"sp": lax.rem(me + d, nsp)}, device_id_type=MESH)
+    for d in range(1, ntp):
+        pl.semaphore_signal(barrier, inc=1, device_id={"tp": lax.rem(mine + d, ntp)}, device_id_type=MESH)
 
     copies = []
     for kind, (source, held) in enumerate(((decay, decay_v), (drive, drive_v), (gate, gate_v))):
@@ -55,12 +61,6 @@
         copies[2][j].start()
     gain_copy = pltpu.make_async_copy(gain, gain_v, gain_sem)
     gain_copy.start()
-
-    barrier = pltpu.get_barrier_semaphore()
-    for d in range(1, nsp):
-        pl.semaphore_signal(barrier, inc=1, device_id={"sp": lax.rem(me + d, nsp)}, device_id_type=MESH)
-    for d in range(1, ntp):
-        pl.semaphore_signal(barrier, inc=1, device_id={"tp": lax.rem(mine + d, ntp)}, device_id_type=MESH)
 
     row = lax.broadcasted_iota(jnp.int32, (SUB, LANES), 0)
     zero = jnp.zeros((SUB, LANES), jnp.float32)
@@ -205,6 +205,16 @@
         ))
     for copy in sends:
         copy.start()
+    gain_copy.wait()
+
+    def weigh(j, carry):
+        own = gain_v[pl.ds(j, 1), :]
+        for _, apart in chunks:
+            gated_s[j, apart, :] = gated_s[j, apart, :] * own
+        return carry
+
+    lax.fori_loop(0, tiles, weigh, 0)
+
     for copy in sends:
         copy.wait()
 
@@ -212,20 +222,28 @@
     for s in range(1, ntp):
         power = power + powers[s]
     power = power * (1.0 / (length * channels * ntp))
-    inverse = lax.rsqrt(power + 1e-06) * length ** (-0.5)
+    inverse[...] = lax.rsqrt(power + 1e-06) * length ** (-0.5)
+
+
+def emit(gated, inverse, out, inv_s, staged, sems):
+    rows, channels = out.shape
+    tiles = channels // LANES
+    steps = rows // SUB
+    pitch = spaced(steps)
+    scale = inverse[...]
     for k in range(steps):
-        inv_s[at(k), :] = jnp.broadcast_to(inverse[:, k : k + 1], (SUB, LANES))
-
-    gain_copy.wait()
-
-    def emit(j, carry):
-        columns = pl.ds(pl.multiple_of(j * LANES, LANES), LANES)
-        own = gain_v[pl.ds(j, 1), :]
-        for dense, apart in chunks:
-            out[dense, columns] = (gated_s[j, apart, :] * inv_s[apart, :] * own).astype(jnp.bfloat16)
-        return carry
-
-    lax.fori_loop(0, tiles, emit, 0)
+        inv_s[pl.ds(k, SUB, stride=pitch), :] = jnp.broadcast_to(scale[:, k : k + 1], (SUB, LANES))
+    copies = []
+    for i in range(SUB):
+        dense, apart = pl.ds(i * steps, steps), pl.ds(i * pitch, steps)
+        for j in range(tiles):
+            staged[dense, pl.ds(j * LANES, LANES)] = (
+                gated[j, apart, :] * inv_s[apart, :]
+            ).astype(jnp.bfloat16)
+        copies.append(pltpu.make_async_copy(staged.at[dense], out.at[dense], sems.at[i]))
+        copies[-1].start()
+    for copy in copies:
+        copy.wait()
 
 
 def body(nsp, ntp, decay_rate, drive_in, gate_in, norm_gain):
@@ -238,14 +256,16 @@
     half = pltpu.VMEM((tiles, rows, LANES), jnp.bfloat16)
     outside = pl.BlockSpec(memory_space=pltpu.HBM)
     vmem = pl.BlockSpec(memory_space=pltpu.VMEM)
-    result = pl.pallas_call(
+    gated, inverse = pl.pallas_call(
         functools.partial(kernel, nsp, ntp),
-        out_shape=jax.ShapeDtypeStruct((rows, channels), jnp.bfloat16),
+        out_shape=(
+            pltpu.VMEM((tiles, SUB * spaced(steps), LANES), jnp.float32),
+            pltpu.VMEM((SUB, width), jnp.float32),
+        ),
         in_specs=[outside] * 4,
-        out_specs=vmem,
+        out_specs=(vmem, vmem),
         scratch_shapes=[
-            plane, half, half, wide, wide, wide, plane, plane, plane, wide,
-            pltpu.VMEM((SUB * spaced(steps), LANES), jnp.float32),
+            plane, half, half, wide, wide, wide, plane, plane, plane,
             pltpu.VMEM((4, tiles, SUB, LANES), jnp.float32),
             pltpu.VMEM((nsp, 3, tiles, LANES), jnp.float32),
             pltpu.VMEM((ntp, SUB, width), jnp.float32),
@@ -269,6 +289,21 @@
             norm_gain.reshape(tiles, LANES),
         )
     ))
+    result = pl.pallas_call(
+        emit,
+        out_shape=jax.ShapeDtypeStruct((rows, channels), jnp.bfloat16),
+        in_specs=[vmem, vmem],
+        out_specs=outside,
+        scratch_shapes=[
+            pltpu.VMEM((SUB * spaced(steps), LANES), jnp.float32),
+            pltpu.VMEM((rows, channels), jnp.bfloat16),
+            pltpu.SemaphoreType.DMA((SUB,)),
+        ],
+        compiler_params=pltpu.CompilerParams(vmem_limit_bytes=32 * 1024 * 1024),
+    )(
+        pltpu.with_memory_space_constraint(gated, pltpu.VMEM),
+        pltpu.with_memory_space_constraint(inverse, pltpu.VMEM),
+    )
     return result.reshape(batch, rows, channels)
 
 

time: 16.2 us -> 16 us (0.988)
  local copies, waits for them, and re-layouts: 0.97 us -> 0 us
  Pallas kernels: 15.1 us -> 15.8 us
    unnamed x1 -> x0, local copies, waits for them, and re-layouts: 0.97 us -> none
    pallas_call x1 -> x2, Pallas kernels: 15.1 us -> 15.8 us  [the longest x1 14.5 us: body(): pl.pallas_call(functools.partial(kernel, nsp, ntp), out_shape=(pltpu.VMEM...]
where the time goes in v4:
time: 16 us; the launch traced here: 15.8 us
  Pallas kernels  15.8 us (99%)
    pallas_call x1, Pallas kernels, body(): pl.pallas_call(functools.partial(kernel, nsp, ntp), out_shape=(pltpu.VMEM...  14.5 us
    pallas_call x1, Pallas kernels, body(): pl.pallas_call(emit, out_shape=jax.ShapeDtypeStruct((rows, channels), jnp...  1.25 us

profile of v4, /device:TPU:0, one launch (start us, length us, event | category | flops | bytes accessed | tf_op | source)
XLA Modules:
  0.0 15.8 jit_solution(8370999581614616682)
XLA Ops:
  0.0 14.5 %shard_map.46 = (f32[8,544,128]{2,1,0:T(8,128)S(1)}, f32[8,128]{1,0:T(8,128)S(1)}) custom-call(f32[512,1024]{1,0:T(8,128)} %bitcast.5, bf16[512,1024]{1,0:T(8,128)(2,1)} %bitcast.6, bf16[512,1024]{1,0:T(8,128)(2,1)} %bitcast.7, f32[8,128]{1,0:T(8,128)} %bitcast.8), custom_call_target="tpu_custom_call" | custom-call | tf_op jit(solution)/shard_map/pallas_call | solution.py:259
  14.6 1.3 %shard_map.47 = bf16[512,1024]{1,0:T(8,128)(2,1)} custom-call(f32[8,544,128]{2,1,0:T(8,128)S(1)} %get-tuple-element.7.gated, f32[8,128]{1,0:T(8,128)S(1)} %get-tuple-element.8.inverse), custom_call_target="tpu_custom_call" | custom-call | tf_op jit(solution)/shard_map/pallas_call | solution.py:292

commit v5 on v4

--- a/solution.py
+++ b/solution.py
@@ -41,8 +41,12 @@
     me, mine = lax.axis_index("sp"), lax.axis_index("tp")
 
     barrier = pltpu.get_barrier_semaphore()
-    for d in range(1, nsp):
-        pl.semaphore_signal(barrier, inc=1, device_id={"sp": lax.rem(me + d, nsp)}, device_id_type=MESH)
+    ahead_first = (2 * me + 1) // nsp
+    for i in range(nsp - 1):
+        high = nsp - 1 - i - (i + me + 1) // nsp
+        low = i + (nsp - 1 - me + i + 1) // nsp
+        peer = high * (1 - ahead_first) + low * ahead_first
+        pl.semaphore_signal(barrier, inc=1, device_id={"sp": peer}, device_id_type=MESH)
     for d in range(1, ntp):
         pl.semaphore_signal(barrier, inc=1, device_id={"tp": lax.rem(mine + d, ntp)}, device_id_type=MESH)
 
@@ -191,10 +195,10 @@
             squares = squares + gated * gated
         return jnp.where(lane == k, jnp.sum(squares, axis=1, keepdims=True), sums)
 
-    powers[mine] = unrolled(steps, 8, finish, jnp.zeros((SUB, width), jnp.float32))
+    powers[mine] = unrolled(steps, 64, finish, jnp.zeros((SUB, width), jnp.float32))
 
     sends = []
-    for d in range(1, ntp):
+    for d in sorted(range(1, ntp), key=lambda d: abs(2 * d - ntp)):
         sends.append(pltpu.make_async_remote_copy(
             src_ref=powers.at[mine],
             dst_ref=powers.at[mine],

time: 16 us -> 15.3 us (0.956)
  Pallas kernels: 15.8 us -> 15.2 us
    pallas_call x1, Pallas kernels: 14.5 us -> 13.9 us  [body(): pl.pallas_call(functools.partial(kernel, nsp, ntp), out_shape=(pltpu.VMEM...]
where the time goes in v5:
time: 15.3 us; the launch traced here: 15.2 us
  Pallas kernels  15.2 us (99%)
    pallas_call x1, Pallas kernels, body(): pl.pallas_call(functools.partial(kernel, nsp, ntp), out_shape=(pltpu.VMEM...  13.9 us
    pallas_call x1, Pallas kernels, body(): pl.pallas_call(emit, out_shape=jax.ShapeDtypeStruct((rows, channels), jnp...  1.25 us

profile of v5, /device:TPU:0, one launch (start us, length us, event | category | flops | bytes accessed | tf_op | source)
XLA Modules:
  0.0 15.2 jit_solution(246152991427928127)
XLA Ops:
  0.0 13.9 %shard_map.46 = (f32[8,544,128]{2,1,0:T(8,128)S(1)}, f32[8,128]{1,0:T(8,128)S(1)}) custom-call(f32[512,1024]{1,0:T(8,128)} %bitcast.5, bf16[512,1024]{1,0:T(8,128)(2,1)} %bitcast.6, bf16[512,1024]{1,0:T(8,128)(2,1)} %bitcast.7, f32[8,128]{1,0:T(8,128)} %bitcast.8), custom_call_target="tpu_custom_call" | custom-call | tf_op jit(solution)/shard_map/pallas_call | solution.py:263
  13.9 1.3 %shard_map.47 = bf16[512,1024]{1,0:T(8,128)(2,1)} custom-call(f32[8,544,128]{2,1,0:T(8,128)S(1)} %get-tuple-element.7.gated, f32[8,128]{1,0:T(8,128)S(1)} %get-tuple-element.8.inverse), custom_call_target="tpu_custom_call" | custom-call | tf_op jit(solution)/shard_map/pallas_call | solution.py:296
